TPU v7x, 32 devices: a whole 2x2x4 slice. The times are simulated.
32 devices in a mesh: band: 8 (over y, x, core), gslab: 4 (over z).
Axes of the slice: x: 2, y: 2, z: 4, core: 2. Of those that a mesh axis runs over, the one named last changes fastest.
Arguments:
- band_coeffs: float32 [3072, 49152], P('band', 'gslab'), may hold values from -6 to 6
- sign_table: int32 [12, 3072], P(None, 'band'), may hold values from -1 to 1, as said below
- slice_widths: int32 [16], replicated, may hold values from 96 to 384, as said below
- owner_map: int32 [16], replicated, may hold values from 0 to 15, each once
Outputs:
- pseudobands: float32 [192, 49152], P(('band', 'gslab'))
Inputs may be any that keep to these rules, and one draw needn't show every extreme that they name: `sign_table`: every entry is -1 or 1. `slice_widths`: the widths sum to 3072; every slice holds 96 to 384 bands, and in every draw some slice holds exactly 96 and some exactly 384. `owner_map`: each slice appears once.
All inputs are finite; a program needn't handle non-finite values.
Results may differ from a plain program's by a relative error of at most 0.0003.
Values sent between devices are 32-bit elements; how exact they have to be, the bound alone decides.
A program may use at most 128 MiB of HBM per device.

v0:
```python
import functools

import jax
import jax.numpy as jnp
from jax import lax
from jax.experimental import pallas as pl
from jax.experimental.pallas import tpu as pltpu
from jax.sharding import PartitionSpec as P

NARROWEST = 96
LANES = 128
PIECES = (8, 4, 2, 1)
MERGE_LAG = 2
FINISH_LAG = 4
MESH = pl.DeviceIdType.MESH


def mixing_rows(row_ids, slice_of_band, sign_float, owner_map, inverse, per_slice):
    slice_count = owner_map.shape[0]
    slot_group = row_ids // per_slice
    within = row_ids % per_slice
    slice_range = jnp.arange(slice_count, dtype=jnp.int32)
    picked = slot_group[:, None] == slice_range[None, :]
    target = jnp.sum(jnp.where(picked, owner_map[None, :], 0), axis=1)
    member = target[:, None] == slice_range[None, :]
    row_scale = jnp.sum(jnp.where(member, inverse[None, :], 0.0), axis=1)
    one_hot = (within[:, None] == jnp.arange(per_slice, dtype=jnp.int32)[None, :]).astype(
        jnp.float32
    )
    sign_rows = jnp.dot(
        one_hot, sign_float, precision=lax.Precision.HIGHEST, preferred_element_type=jnp.float32
    )
    return jnp.where(slice_of_band[None, :] == target[:, None], sign_rows * row_scale[:, None], 0.0)


def dense(band_coeffs, sign_table, slice_widths, owner_map):
    local_bands = band_coeffs.shape[0]
    per_slice = sign_table.shape[0]
    slice_count = owner_map.shape[0]
    total_rows = slice_count * per_slice
    first_band = lax.axis_index("band") * local_bands
    band_ids = first_band + jnp.arange(local_bands, dtype=jnp.int32)
    ends = jnp.cumsum(slice_widths)
    slice_of_band = jnp.sum((band_ids[:, None] >= ends[None, :]).astype(jnp.int32), axis=1)
    inverse = 1.0 / jnp.sqrt(slice_widths.astype(jnp.float32))
    sign_float = sign_table.astype(jnp.float32)
    row_ids = jnp.arange(total_rows, dtype=jnp.int32)
    mixing = mixing_rows(row_ids, slice_of_band, sign_float, owner_map, inverse, per_slice)
    summed = lax.psum_scatter(
        jnp.dot(
            mixing, band_coeffs, precision=lax.Precision.HIGHEST, preferred_element_type=jnp.float32
        ),
        "band",
        scatter_dimension=0,
        tiled=True,
    )
    return lax.all_to_all(summed, "gslab", split_axis=0, concat_axis=1, tiled=True)


def two_term_dot(exact, values):
    high = values.astype(jnp.bfloat16)
    low = (values - high.astype(jnp.float32)).astype(jnp.bfloat16)
    return jnp.dot(exact, high, preferred_element_type=jnp.float32) + jnp.dot(
        exact, low, preferred_element_type=jnp.float32
    )


def kernel(
    slabs, pieces, reach,
    widths_ref, owner_ref, signs_ref, band_ref, out_ref,
    held, mix, sent, got, chosen, scale, half, came, done,
    load_sem, send1, recv1, send2, recv2, send3, recv3,
):
    my_group = lax.axis_index("band")
    my_slab = lax.axis_index("gslab")
    my_core = lax.rem(my_group, 2)
    bits = (my_group // 4, lax.rem(my_group // 2, 2))
    devices = 8 * slabs
    me = my_group * slabs + my_slab
    per_slice, local_bands = signs_ref.shape
    slices = widths_ref.shape[0]
    packed, width = sent.shape[2:]
    mine = done.shape[2]
    peers = done.shape[1]
    live = reach * per_slice
    total = 4 * pieces

    def group_of(axis, along, other, core):
        return along * 4 + other * 2 + core if axis == 0 else other * 4 + along * 2 + core

    def own(axis):
        return bits[axis], bits[1 - axis]

    def quarter_at(axis, k):
        return lax.rem(own(axis)[0] * 2 + my_core + 1 + k, 4)

    def load(part, quarter):
        index = quarter * pieces + part
        return pltpu.make_async_copy(
            band_ref.at[:, pl.ds(pl.multiple_of(index * width, width), width)],
            held.at[index],
            load_sem.at[index],
        )

    def load_piece(part):
        for k in range(4):
            load(part, quarter_at(part % 2, k)).start()

    load_piece(0)
    barrier = pltpu.get_barrier_semaphore()

    @pl.loop(1, devices)
    def _(k):
        other = lax.rem(me + k, devices)
        pl.semaphore_signal(
            barrier, inc=1,
            device_id={"band": other // slabs, "gslab": lax.rem(other, slabs)},
            device_id_type=MESH,
        )

    ends = []
    running = jnp.int32(0)
    for s in range(slices):
        running = running + widths_ref[s]
        ends.append(running)

    first_band = my_group * local_bands
    bands = first_band + lax.broadcasted_iota(jnp.int32, (1, local_bands), 1)
    slice_of = jnp.zeros((1, local_bands), jnp.int32)
    first = jnp.int32(0)
    for s in range(slices):
        slice_of = slice_of + jnp.where(bands >= ends[s], 1, 0)
        first = first + jnp.where(first_band >= ends[s], 1, 0)
    row = lax.broadcasted_iota(jnp.int32, (packed, per_slice), 0)
    column = lax.broadcasted_iota(jnp.int32, (packed, per_slice), 1)
    repeat = jnp.where(lax.rem(row, per_slice) == column, 1.0, 0.0).astype(jnp.float32)
    signs = jnp.dot(
        repeat, signs_ref[...].astype(jnp.float32), preferred_element_type=jnp.float32
    )
    row = lax.broadcasted_iota(jnp.int32, (packed, local_bands), 0)
    hit = (slice_of - first == row // per_slice) & (row < live)
    mix[...] = jnp.where(hit, signs, 0.0).astype(jnp.bfloat16)

    def exchange(part, quarter, source):
        axis = part % 2
        return pltpu.make_async_remote_copy(
            src_ref=sent.at[part, quarter],
            dst_ref=got.at[part, source],
            send_sem=send1.at[part, quarter],
            recv_sem=recv1.at[part, source],
            device_id={
                "band": group_of(axis, quarter // 2, own(axis)[1], lax.rem(quarter, 2)),
                "gslab": my_slab,
            },
            device_id_type=MESH,
        )

    def partial_sums(part, quarter):
        load(part, quarter).wait()
        return two_term_dot(mix[...], held[quarter * pieces + part])

    def send_partial(part):
        if part + 1 < pieces:
            load_piece(part + 1)
        here = own(part % 2)[0] * 2 + my_core

        @pl.loop(0, 3)
        def _(k):
            quarter = quarter_at(part % 2, k)
            sent[part, quarter] = partial_sums(part, quarter)
            exchange(part, quarter, here).start()

        got[part, here] = partial_sums(part, here)

    def cross(part):
        axis = part % 2
        along, other = own(axis)
        return pltpu.make_async_remote_copy(
            src_ref=half.at[part, 0],
            dst_ref=came.at[part],
            send_sem=send2.at[part],
            recv_sem=recv2.at[part],
            device_id={"band": group_of(axis, along, 1 - other, my_core), "gslab": my_slab},
            device_id_type=MESH,
        )

    def merge(part):
        axis = part % 2

        @pl.loop(0, 3)
        def _(k):
            source = quarter_at(axis, k)
            exchange(part, source, source).wait_recv()

        rows = got[part].reshape(4 * packed, width)
        value = two_term_dot(chosen[axis], rows)
        half[part] = value.reshape(2, peers * mine, width)
        cross(part).start()

    def here_of(axis):
        return (own(axis)[0] * 2 + my_core) * slabs + my_slab

    def columns(part, peer):
        start = lax.rem(peer, slabs) * (total * width) + ((peer // slabs) * pieces + part) * width
        return out_ref.at[:, pl.ds(pl.multiple_of(start, width), width)]

    def deliver(part, peer, source):
        axis = part % 2
        quarter = peer // slabs
        return pltpu.make_async_remote_copy(
            src_ref=done.at[part, peer],
            dst_ref=columns(part, source),
            send_sem=send3.at[part, peer],
            recv_sem=recv3.at[part, source],
            device_id={
                "band": group_of(axis, quarter // 2, own(axis)[1], lax.rem(quarter, 2)),
                "gslab": lax.rem(peer, slabs),
            },
            device_id_type=MESH,
        )

    def keep(part):
        here = here_of(part % 2)
        return pltpu.make_async_copy(done.at[part, here], columns(part, here), recv3.at[part, here])

    def finish(part):
        axis = part % 2
        cross(part).wait_recv()
        for peer in range(peers):
            rows = slice(peer * mine, (peer + 1) * mine)
            done[part, peer] = (half[part, 1, rows] + came[part, rows]) * scale[axis, rows, :1]
        keep(part).start()
        here = here_of(axis)

        @pl.loop(1, peers)
        def _(k):
            deliver(part, lax.rem(here + k, peers), here).start()

    pl.semaphore_wait(barrier, devices - 1)
    send_partial(0)

    for axis in range(2):
        along, other = own(axis)
        shape = (2 * peers * mine, 1)
        tall = lax.broadcasted_iota(jnp.int32, shape, 0)
        stays = tall // (peers * mine)
        rest = lax.rem(tall, peers * mine)
        peer = rest // mine
        quarter = peer // slabs
        side = jnp.where(stays == 1, other, 1 - other)
        group = group_of(axis, quarter // 2, side, lax.rem(quarter, 2))
        output_row = (group * slabs + lax.rem(peer, slabs)) * mine + lax.rem(rest, mine)
        block = output_row // per_slice
        target = jnp.zeros(shape, jnp.int32)
        for s in range(slices):
            target = jnp.where(block == s, owner_ref[s], target)
        breadth = jnp.ones(shape, jnp.int32)
        for s in range(slices):
            breadth = jnp.where(target == s, widths_ref[s], breadth)
        root = 1.0 / jnp.sqrt(breadth.astype(jnp.float32))
        scale[axis] = jnp.broadcast_to(root[peers * mine:], (peers * mine, LANES))
        wanted = target * per_slice + lax.rem(output_row, per_slice)
        wide = lax.broadcasted_iota(jnp.int32, (1, 4 * packed), 1)
        place = lax.rem(wide, packed)
        quarter = wide // packed
        begin = group_of(axis, quarter // 2, other, lax.rem(quarter, 2)) * local_bands
        lowest = jnp.zeros((1, 4 * packed), jnp.int32)
        for s in range(slices):
            lowest = lowest + jnp.where(begin >= ends[s], 1, 0)
        offered = jnp.where(place < live, lowest * per_slice + place, -2)
        chosen[axis] = jnp.where(wanted == offered, 1.0, 0.0).astype(jnp.bfloat16)

    for step in range(1, pieces + FINISH_LAG):
        if step < pieces:
            send_partial(step)
        if 0 <= step - MERGE_LAG < pieces:
            merge(step - MERGE_LAG)
        if 0 <= step - FINISH_LAG < pieces:
            finish(step - FINISH_LAG)

    for part in range(pieces):
        cross(part).wait_send()
        here = own(part % 2)[0] * 2 + my_core

        @pl.loop(0, 3)
        def _(k):
            exchange(part, quarter_at(part % 2, k), here).wait_send()

        here = here_of(part % 2)

        @pl.loop(1, peers)
        def _(k):
            peer = lax.rem(here + k, peers)
            deliver(part, peer, peer).wait()

        keep(part).wait()


def on_device(groups, slabs, band_coeffs, sign_table, slice_widths, owner_map):
    local_bands, local_columns = band_coeffs.shape
    per_slice = sign_table.shape[0]
    rows = owner_map.shape[0] * per_slice
    share, odd = divmod(local_columns, 4 * LANES)
    if groups != 8 or odd or rows % (8 * slabs):
        return dense(band_coeffs, sign_table, slice_widths, owner_map)
    pieces = next(p for p in PIECES if share % p == 0)
    width = share // pieces * LANES
    reach = (local_bands - 2) // NARROWEST + 2
    packed = -(-reach * per_slice // 8) * 8
    mine = rows // (8 * slabs)
    peers = 4 * slabs
    return pl.pallas_call(
        functools.partial(kernel, slabs, pieces, reach),
        out_shape=jax.ShapeDtypeStruct((mine, local_columns * slabs), jnp.float32),
        in_specs=[
            pl.BlockSpec(memory_space=pltpu.SMEM),
            pl.BlockSpec(memory_space=pltpu.SMEM),
            pl.BlockSpec(memory_space=pltpu.VMEM),
            pl.BlockSpec(memory_space=pl.ANY),
        ],
        out_specs=pl.BlockSpec(memory_space=pl.ANY),
        scratch_shapes=[
            pltpu.VMEM((4 * pieces, local_bands, width), jnp.float32),
            pltpu.VMEM((packed, local_bands), jnp.bfloat16),
            pltpu.VMEM((pieces, 4, packed, width), jnp.float32),
            pltpu.VMEM((pieces, 4, packed, width), jnp.float32),
            pltpu.VMEM((2, 2 * peers * mine, 4 * packed), jnp.bfloat16),
            pltpu.VMEM((2, peers * mine, LANES), jnp.float32),
            pltpu.VMEM((pieces, 2, peers * mine, width), jnp.float32),
            pltpu.VMEM((pieces, peers * mine, width), jnp.float32),
            pltpu.VMEM((pieces, peers, mine, width), jnp.float32),
            pltpu.SemaphoreType.DMA((4 * pieces,)),
            pltpu.SemaphoreType.DMA((pieces, 4)),
            pltpu.SemaphoreType.DMA((pieces, 4)),
            pltpu.SemaphoreType.DMA((pieces,)),
            pltpu.SemaphoreType.DMA((pieces,)),
            pltpu.SemaphoreType.DMA((pieces, peers)),
            pltpu.SemaphoreType.DMA((pieces, peers)),
        ],
        compiler_params=pltpu.CompilerParams(
            collective_id=0, has_side_effects=True, vmem_limit_bytes=60 * 2**20
        ),
        name="pseudobands",
    )(slice_widths, owner_map, sign_table, band_coeffs)


def solution(mesh):
    return jax.shard_map(
        functools.partial(on_device, mesh.shape["band"], mesh.shape["gslab"]),
        mesh=mesh,
        in_specs=(P("band", "gslab"), P(None, "band"), P(), P()),
        out_specs=P(("band", "gslab"), None),
        check_vma=False,
    )
```

profile of v0, /device:TPU:0, one launch (start us, length us, event | category | flops | bytes accessed | tf_op | source)
XLA Modules:
  0.0 61.5 jit_solution(9005165780577675365)
XLA Ops:
  0.0 58.9 %pseudobands.1 = f32[6,49152]{1,0:T(8,128)} custom-call(s32[16]{0:T(128)} %widths_ref.1, s32[16]{0:T(128)} %owner_ref.1, s32[12,384]{1,0:T(8,128)} %signs_ref.1, f32[384,12288]{1,0:T(8,128)} %band_ref.1), custom_call_target="tpu_custom_call" | custom-call | tf_op jit(solution)/shard_map/pseudobands/pallas_call | solution.py:312
  58.9 2.7 %copy.6 = f32[6,49152]{1,0:T(8,128)} copy(f32[6,49152]{1,0:T(8,128)} %pseudobands.1) | data formatting | bytes 2359296
where the time goes:
time: 61.7 us; the launch traced here: 61.5 us
  Pallas kernels  58.9 us (95%)
  local copies, waits for them, and re-layouts  2.65 us (4%)
    pallas_call x1, Pallas kernels, on_device(): pl.pallas_call(functools.partial(kernel, slabs, pieces, reach), out_shape...  58.9 us
    unnamed x1, local copies, waits for them, and re-layouts  2.65 us

commit v1 on v0

v1 whole, which is shorter than its diff:
```python
import functools

import jax
import jax.numpy as jnp
from jax import lax
from jax.experimental import pallas as pl
from jax.experimental.pallas import tpu as pltpu
from jax.sharding import PartitionSpec as P

NARROWEST = 96
LANES = 128
SUBLANES = 8
HALF = 4
VMEM = 67043328
MERGE_LAG = 2
FINISH_LAG = 4
UNPACK_LAG = 8
MESH = pl.DeviceIdType.MESH


def mixing_rows(row_ids, slice_of_band, sign_float, owner_map, inverse, per_slice):
    slice_count = owner_map.shape[0]
    slot_group = row_ids // per_slice
    within = row_ids % per_slice
    slice_range = jnp.arange(slice_count, dtype=jnp.int32)
    picked = slot_group[:, None] == slice_range[None, :]
    target = jnp.sum(jnp.where(picked, owner_map[None, :], 0), axis=1)
    member = target[:, None] == slice_range[None, :]
    row_scale = jnp.sum(jnp.where(member, inverse[None, :], 0.0), axis=1)
    one_hot = (within[:, None] == jnp.arange(per_slice, dtype=jnp.int32)[None, :]).astype(
        jnp.float32
    )
    sign_rows = jnp.dot(
        one_hot, sign_float, precision=lax.Precision.HIGHEST, preferred_element_type=jnp.float32
    )
    return jnp.where(slice_of_band[None, :] == target[:, None], sign_rows * row_scale[:, None], 0.0)


def dense(band_coeffs, sign_table, slice_widths, owner_map):
    local_bands = band_coeffs.shape[0]
    per_slice = sign_table.shape[0]
    slice_count = owner_map.shape[0]
    total_rows = slice_count * per_slice
    first_band = lax.axis_index("band") * local_bands
    band_ids = first_band + jnp.arange(local_bands, dtype=jnp.int32)
    ends = jnp.cumsum(slice_widths)
    slice_of_band = jnp.sum((band_ids[:, None] >= ends[None, :]).astype(jnp.int32), axis=1)
    inverse = 1.0 / jnp.sqrt(slice_widths.astype(jnp.float32))
    sign_float = sign_table.astype(jnp.float32)
    row_ids = jnp.arange(total_rows, dtype=jnp.int32)
    mixing = mixing_rows(row_ids, slice_of_band, sign_float, owner_map, inverse, per_slice)
    summed = lax.psum_scatter(
        jnp.dot(
            mixing, band_coeffs, precision=lax.Precision.HIGHEST, preferred_element_type=jnp.float32
        ),
        "band",
        scatter_dimension=0,
        tiled=True,
    )
    return lax.all_to_all(summed, "gslab", split_axis=0, concat_axis=1, tiled=True)


def two_term_dot(exact, values):
    high = values.astype(jnp.bfloat16)
    low = (values - high.astype(jnp.float32)).astype(jnp.bfloat16)
    return jnp.dot(exact, high, preferred_element_type=jnp.float32) + jnp.dot(
        exact, low, preferred_element_type=jnp.float32
    )


def kernel(
    slabs, chunks, reach,
    widths_ref, owner_ref, signs_ref, band_ref, out_ref,
    held, mix, sent, got, chosen, scale, half, came, done, parcel,
    load_sem, send1, recv1, send2, recv2, send3, recv3, near,
):
    my_group = lax.axis_index("band")
    my_slab = lax.axis_index("gslab")
    my_core = lax.rem(my_group, 2)
    bits = (my_group // 4, lax.rem(my_group // 2, 2))
    per_slice, local_bands = signs_ref.shape
    slices = widths_ref.shape[0]
    packed, width = sent.shape[2:]
    peers = done.shape[1]
    mine = out_ref.shape[0]
    extra = mine - HALF
    tall_block = mine * slabs
    tiles = slabs - 1
    live = reach * per_slice

    def group_of(axis, along, other, core):
        return along * 4 + other * 2 + core if axis == 0 else other * 4 + along * 2 + core

    def own(axis):
        return bits[axis], bits[1 - axis]

    def here_at(axis):
        return own(axis)[0] * 2 + my_core

    def quarter_at(axis, k):
        return lax.rem(own(axis)[0] * 2 + 2 + k // 2 * 2, 4) + lax.rem(my_core + k + k // 2, 2)

    def load(chunk, quarter):
        start = (quarter * chunks + chunk) * width
        return pltpu.make_async_copy(
            band_ref.at[:, pl.ds(pl.multiple_of(start, width), width)],
            held.at[chunk, quarter],
            load_sem.at[chunk % 3],
        )

    def load_chunk(chunk):
        for quarter in range(4):
            load(chunk, quarter).start()

    def wait_load(chunk):
        pltpu.make_async_copy(held.at[chunk], held.at[chunk], load_sem.at[chunk % 3]).wait()

    load_chunk(0)

    barrier = pltpu.get_barrier_semaphore()

    def greet(semaphore, group, slab):
        pl.semaphore_signal(
            semaphore, inc=1, device_id={"band": group, "gslab": slab}, device_id_type=MESH
        )

    inner = lax.rem(my_slab + slabs - 1, slabs) // tiles
    outer = my_slab // tiles
    sides = 2 - inner - outer

    def greet_sides(semaphore):
        @pl.when(my_slab > 0)
        def _():
            greet(semaphore, my_group, my_slab - 1)

        @pl.when(my_slab < slabs - 1)
        def _():
            greet(semaphore, my_group, my_slab + 1)

    greet(barrier, group_of(0, bits[0], bits[1], 1 - my_core), my_slab)
    for axis in range(2):
        along, other = own(axis)
        for core in range(2):
            greet(barrier, group_of(axis, 1 - along, other, core), my_slab)
    greet_sides(barrier)
    load_chunk(1)

    ends = []
    running = jnp.int32(0)
    for s in range(slices):
        running = running + widths_ref[s]
        ends.append(running)

    first_band = my_group * local_bands
    bands = first_band + lax.broadcasted_iota(jnp.int32, (1, local_bands), 1)
    slice_of = jnp.zeros((1, local_bands), jnp.int32)
    first = jnp.int32(0)
    for s in range(slices):
        slice_of = slice_of + jnp.where(bands >= ends[s], 1, 0)
        first = first + jnp.where(first_band >= ends[s], 1, 0)
    row = lax.broadcasted_iota(jnp.int32, (packed, per_slice), 0)
    column = lax.broadcasted_iota(jnp.int32, (packed, per_slice), 1)
    repeat = jnp.where(lax.rem(row, per_slice) == column, 1.0, 0.0).astype(jnp.float32)
    signs = jnp.dot(
        repeat, signs_ref[...].astype(jnp.float32), preferred_element_type=jnp.float32
    )
    row = lax.broadcasted_iota(jnp.int32, (packed, local_bands), 0)
    hit = (slice_of - first == row // per_slice) & (row < live)
    mix[...] = jnp.where(hit, signs, 0.0).astype(jnp.bfloat16)

    def exchange(chunk, quarter, source):
        axis = chunk % 2
        return pltpu.make_async_remote_copy(
            src_ref=sent.at[chunk, quarter],
            dst_ref=got.at[chunk, source],
            send_sem=send1,
            recv_sem=recv1.at[chunk],
            device_id={
                "band": group_of(axis, quarter // 2, own(axis)[1], lax.rem(quarter, 2)),
                "gslab": my_slab,
            },
            device_id_type=MESH,
        )

    def send_partial(chunk):
        if chunk + 2 < chunks:
            load_chunk(chunk + 2)
        wait_load(chunk)
        axis = chunk % 2
        here = here_at(axis)

        @pl.loop(0, 3)
        def _(k):
            quarter = quarter_at(axis, k)
            sent[chunk, quarter] = two_term_dot(mix[...], held[chunk, quarter])
            if chunk:
                exchange(chunk, quarter, here).start()

        got[chunk, here] = two_term_dot(mix[...], held[chunk, here])

    def cross(chunk):
        axis = chunk % 2
        along, other = own(axis)
        return pltpu.make_async_remote_copy(
            src_ref=half.at[chunk, 0],
            dst_ref=came.at[chunk],
            send_sem=send2,
            recv_sem=recv2.at[chunk],
            device_id={"band": group_of(axis, along, 1 - other, my_core), "gslab": my_slab},
            device_id_type=MESH,
        )

    def wait_bytes(ref, semaphore):
        pltpu.make_async_copy(ref, ref, semaphore).wait()

    def merge(chunk):
        wait_bytes(got.at[chunk, pl.ds(0, 3)], recv1.at[chunk])
        rows = got[chunk].reshape(4 * packed, width)
        value = two_term_dot(chosen[chunk % 2], rows)
        half[chunk] = value.reshape(2, peers * mine, width)
        cross(chunk).start()

    def deliver(chunk, slab, quarter):
        axis = chunk % 2
        return pltpu.make_async_remote_copy(
            src_ref=done.at[chunk, quarter * slabs + slab],
            dst_ref=parcel.at[my_slab, here_at(axis), chunk],
            send_sem=send3,
            recv_sem=recv3.at[chunk],
            device_id={
                "band": group_of(axis, quarter // 2, own(axis)[1], lax.rem(quarter, 2)),
                "gslab": slab,
            },
            device_id_type=MESH,
        )

    def finish(chunk):
        axis = chunk % 2
        here = here_at(axis)
        cross(chunk).wait_recv()
        total = (half[chunk, 1] + came[chunk]) * scale[axis, :, :1]
        total = total.reshape(4 * tiles, SUBLANES, width)
        level = lax.broadcasted_iota(jnp.int32, (SUBLANES, LANES), 0)
        early = level % HALF < extra
        for quarter in range(4):
            tile = [total[quarter * tiles + k] for k in range(tiles)]
            left = [t[:, :LANES] for t in tile]
            right = [t[:, LANES:] for t in tile]
            even = jnp.where(early, left[-1], pltpu.roll(right[-1], extra, 0))
            odd = jnp.where(early, pltpu.roll(left[-1], SUBLANES - extra, 0), right[-1])
            for slab in range(slabs):
                at = slab % 2 * HALF
                end = slab // 2 * HALF
                peer = quarter * slabs + slab
                done[chunk, peer, 0] = left[slab // 2][at:at + HALF]
                done[chunk, peer, 1] = right[slab // 2][at:at + HALF]
                done[chunk, peer, 2] = (odd if slab % 2 else even)[end:end + HALF]
        pltpu.make_async_copy(
            done.at[chunk, here * slabs + my_slab], parcel.at[my_slab, here, chunk], recv3.at[chunk]
        ).start()
        side = my_slab // 2

        @pl.loop(0, 8)
        def _(k):
            deliver(chunk, 2 - 2 * side + k // 4, lax.rem(here + k, 4)).start()

        @pl.loop(0, 4)
        def _(k):
            deliver(chunk, 4 * side + 1 - my_slab, lax.rem(here + k, 4)).start()

        @pl.loop(1, 4)
        def _(k):
            deliver(chunk, my_slab, lax.rem(here + k, 4)).start()

    def unpack(chunk):
        wait_bytes(parcel.at[:, :, chunk], recv3.at[chunk])
        for slab in range(slabs):
            for quarter in range(4):
                at = ((slab * 4 + quarter) * chunks + chunk) * width
                left, right = slice(at, at + LANES), slice(at + LANES, at + 2 * LANES)
                out_ref[:HALF, left] = parcel[slab, quarter, chunk, 0]
                out_ref[:HALF, right] = parcel[slab, quarter, chunk, 1]
                out_ref[HALF:, left] = parcel[slab, quarter, chunk, 2, :extra]
                out_ref[HALF:, right] = parcel[slab, quarter, chunk, 2, extra:]

    send_partial(0)
    pl.semaphore_wait(barrier, 5 + sides)

    @pl.loop(0, 3)
    def _(k):
        exchange(0, quarter_at(0, k), here_at(0)).start()

    greet_sides(near.at[0])

    for axis in range(2):
        along, other = own(axis)
        shape = (2 * peers * mine, 1)
        tall = lax.broadcasted_iota(jnp.int32, shape, 0)
        stays = tall // (peers * mine)
        rest = lax.rem(tall, peers * mine)
        quarter = rest // tall_block
        rest = lax.rem(rest, tall_block)
        low = rest < slabs * HALF
        beyond = rest - slabs * HALF
        slab = jnp.where(low, rest // HALF, beyond // extra)
        within = jnp.where(low, lax.rem(rest, HALF), HALF + lax.rem(beyond, extra))
        side = jnp.where(stays == 1, other, 1 - other)
        group = group_of(axis, quarter // 2, side, lax.rem(quarter, 2))
        output_row = (group * slabs + slab) * mine + within
        block = output_row // per_slice
        target = jnp.zeros(shape, jnp.int32)
        for s in range(slices):
            target = jnp.where(block == s, owner_ref[s], target)
        breadth = jnp.ones(shape, jnp.int32)
        for s in range(slices):
            breadth = jnp.where(target == s, widths_ref[s], breadth)
        root = 1.0 / jnp.sqrt(breadth.astype(jnp.float32))
        scale[axis] = jnp.broadcast_to(root[peers * mine:], (peers * mine, LANES))
        wanted = target * per_slice + lax.rem(output_row, per_slice)
        wide = lax.broadcasted_iota(jnp.int32, (1, 4 * packed), 1)
        place = lax.rem(wide, packed)
        quarter = wide // packed
        begin = group_of(axis, quarter // 2, other, lax.rem(quarter, 2)) * local_bands
        lowest = jnp.zeros((1, 4 * packed), jnp.int32)
        for s in range(slices):
            lowest = lowest + jnp.where(begin >= ends[s], 1, 0)
        offered = jnp.where(place < live, lowest * per_slice + place, -2)
        chosen[axis] = jnp.where(wanted == offered, 1.0, 0.0).astype(jnp.bfloat16)

    known = 0

    def learn():
        pl.semaphore_wait(near.at[known], sides)
        if known + 1 < tiles:
            greet_sides(near.at[known + 1])

    for step in range(1, chunks + UNPACK_LAG):
        if step < chunks:
            send_partial(step)
        if known < tiles:
            learn()
            known += 1
        if 0 <= step - MERGE_LAG < chunks:
            merge(step - MERGE_LAG)
        if 0 <= step - FINISH_LAG < chunks:
            finish(step - FINISH_LAG)
        if 0 <= step - UNPACK_LAG < chunks:
            unpack(step - UNPACK_LAG)

    wait_bytes(sent.at[:, pl.ds(0, 3)], send1)
    wait_bytes(came, send2)
    wait_bytes(done.at[:, pl.ds(0, peers - 1)], send3)


def on_device(groups, slabs, band_coeffs, sign_table, slice_widths, owner_map):
    local_bands, local_columns = band_coeffs.shape
    per_slice = sign_table.shape[0]
    rows = owner_map.shape[0] * per_slice
    width = 2 * LANES
    chunks, odd = divmod(local_columns, 4 * width)
    mine = rows // (8 * slabs)
    fits = 2 * (mine - HALF) == HALF and slabs == HALF
    if groups != 8 or odd or rows % (8 * slabs) or not fits:
        return dense(band_coeffs, sign_table, slice_widths, owner_map)
    reach = (local_bands - 2) // NARROWEST + 2
    packed = -(-reach * per_slice // 8) * 8
    peers = 4 * slabs
    return pl.pallas_call(
        functools.partial(kernel, slabs, chunks, reach),
        out_shape=pltpu.VMEM((mine, local_columns * slabs), jnp.float32),
        in_specs=[
            pl.BlockSpec(memory_space=pltpu.SMEM),
            pl.BlockSpec(memory_space=pltpu.SMEM),
            pl.BlockSpec(memory_space=pltpu.VMEM),
            pl.BlockSpec(memory_space=pl.ANY),
        ],
        out_specs=pl.BlockSpec(memory_space=pltpu.VMEM),
        scratch_shapes=[
            pltpu.VMEM((chunks, 4, local_bands, width), jnp.float32),
            pltpu.VMEM((packed, local_bands), jnp.bfloat16),
            pltpu.VMEM((chunks, 4, packed, width), jnp.float32),
            pltpu.VMEM((chunks, 4, packed, width), jnp.float32),
            pltpu.VMEM((2, 2 * peers * mine, 4 * packed), jnp.bfloat16),
            pltpu.VMEM((2, peers * mine, LANES), jnp.float32),
            pltpu.VMEM((chunks, 2, peers * mine, width), jnp.float32),
            pltpu.VMEM((chunks, peers * mine, width), jnp.float32),
            pltpu.VMEM((chunks, peers, 3, HALF, LANES), jnp.float32),
            pltpu.VMEM((slabs, 4, chunks, 3, HALF, LANES), jnp.float32),
            pltpu.SemaphoreType.DMA((3,)),
            pltpu.SemaphoreType.DMA,
            pltpu.SemaphoreType.DMA((chunks,)),
            pltpu.SemaphoreType.DMA,
            pltpu.SemaphoreType.DMA((chunks,)),
            pltpu.SemaphoreType.DMA,
            pltpu.SemaphoreType.DMA((chunks,)),
            pltpu.SemaphoreType.REGULAR((slabs - 1,)),
        ],
        compiler_params=pltpu.CompilerParams(
            collective_id=0, has_side_effects=True, vmem_limit_bytes=VMEM - 8 * local_columns * slabs * 4
        ),
        name="pseudobands",
    )(slice_widths, owner_map, sign_table, band_coeffs)


def solution(mesh):
    return jax.shard_map(
        functools.partial(on_device, mesh.shape["band"], mesh.shape["gslab"]),
        mesh=mesh,
        in_specs=(P("band", "gslab"), P(None, "band"), P(), P()),
        out_specs=P(("band", "gslab"), None),
        check_vma=False,
    )
```

time: 61.7 us -> 52.5 us (0.85)
  Pallas kernels: 58.9 us -> 51.2 us
  local copies, waits for them, and re-layouts: 2.65 us -> 1.15 us
    pallas_call x1, Pallas kernels: 58.9 us -> 51.2 us  [on_device(): pl.pallas_call(functools.partial(kernel, slabs, chunks, reach), out_shape...]
    unnamed x1, local copies, waits for them, and re-layouts: 2.65 us -> 1.15 us
where the time goes in v1:
time: 52.5 us; the launch traced here: 52.4 us
  Pallas kernels  51.2 us (98%)
  local copies, waits for them, and re-layouts  1.15 us (2%)
    pallas_call x1, Pallas kernels, on_device(): pl.pallas_call(functools.partial(kernel, slabs, chunks, reach), out_shape...  51.2 us
    unnamed x1, local copies, waits for them, and re-layouts  1.15 us

profile of v1, /device:TPU:0, one launch (start us, length us, event | category | flops | bytes accessed | tf_op | source)
XLA Modules:
  0.0 52.4 jit_solution(2876762774876038253)
XLA Ops:
  0.0 51.2 %pseudobands.1 = f32[6,49152]{1,0:T(8,128)S(1)} custom-call(s32[16]{0:T(128)} %widths_ref.1, s32[16]{0:T(128)} %owner_ref.1, s32[12,384]{1,0:T(8,128)} %signs_ref.1, f32[384,12288]{1,0:T(8,128)} %band_ref.1), custom_call_target="tpu_custom_call" | custom-call | tf_op jit(solution)/shard_map/pseudobands/pallas_call | solution.py:368
  51.2 1.1 %copy.6 = f32[6,49152]{1,0:T(8,128)} copy(f32[6,49152]{1,0:T(8,128)S(1)} %pseudobands.1) | data formatting | bytes 2359296

commit v2 on v1

v2 whole, which is shorter than its diff:
```python
import functools

import jax
import jax.numpy as jnp
from jax import lax
from jax.experimental import pallas as pl
from jax.experimental.pallas import tpu as pltpu
from jax.sharding import PartitionSpec as P

NARROWEST = 96
LANES = 128
SUBLANES = 8
HALF = 4
VMEM = 67043328
CHUNK_REFS = ("held", "sent", "got", "half", "came", "done", "parcel")
NARROW = 2
MERGE_LAG = 2
FINISH_LAG = 4
UNPACK_LAG = 7
MESH = pl.DeviceIdType.MESH


def mixing_rows(row_ids, slice_of_band, sign_float, owner_map, inverse, per_slice):
    slice_count = owner_map.shape[0]
    slot_group = row_ids // per_slice
    within = row_ids % per_slice
    slice_range = jnp.arange(slice_count, dtype=jnp.int32)
    picked = slot_group[:, None] == slice_range[None, :]
    target = jnp.sum(jnp.where(picked, owner_map[None, :], 0), axis=1)
    member = target[:, None] == slice_range[None, :]
    row_scale = jnp.sum(jnp.where(member, inverse[None, :], 0.0), axis=1)
    one_hot = (within[:, None] == jnp.arange(per_slice, dtype=jnp.int32)[None, :]).astype(
        jnp.float32
    )
    sign_rows = jnp.dot(
        one_hot, sign_float, precision=lax.Precision.HIGHEST, preferred_element_type=jnp.float32
    )
    return jnp.where(slice_of_band[None, :] == target[:, None], sign_rows * row_scale[:, None], 0.0)


def dense(band_coeffs, sign_table, slice_widths, owner_map):
    local_bands = band_coeffs.shape[0]
    per_slice = sign_table.shape[0]
    slice_count = owner_map.shape[0]
    total_rows = slice_count * per_slice
    first_band = lax.axis_index("band") * local_bands
    band_ids = first_band + jnp.arange(local_bands, dtype=jnp.int32)
    ends = jnp.cumsum(slice_widths)
    slice_of_band = jnp.sum((band_ids[:, None] >= ends[None, :]).astype(jnp.int32), axis=1)
    inverse = 1.0 / jnp.sqrt(slice_widths.astype(jnp.float32))
    sign_float = sign_table.astype(jnp.float32)
    row_ids = jnp.arange(total_rows, dtype=jnp.int32)
    mixing = mixing_rows(row_ids, slice_of_band, sign_float, owner_map, inverse, per_slice)
    summed = lax.psum_scatter(
        jnp.dot(
            mixing, band_coeffs, precision=lax.Precision.HIGHEST, preferred_element_type=jnp.float32
        ),
        "band",
        scatter_dimension=0,
        tiled=True,
    )
    return lax.all_to_all(summed, "gslab", split_axis=0, concat_axis=1, tiled=True)


def two_term_dot(exact, values):
    high = values.astype(jnp.bfloat16)
    low = (values - high.astype(jnp.float32)).astype(jnp.bfloat16)
    return jnp.dot(exact, high, preferred_element_type=jnp.float32) + jnp.dot(
        exact, low, preferred_element_type=jnp.float32
    )


class Chunk:
    def __init__(self, index, place, start, tiles, refs):
        self.index, self.axis, self.start, self.tiles = index, index % 2, start, tiles
        self.width = tiles * LANES
        for name, ref in zip(CHUNK_REFS, refs):
            setattr(self, name, ref.at[place])


def kernel(
    slabs, reach,
    widths_hbm, owner_hbm, signs_hbm, band_ref, out_ref,
    widths_ref, owner_ref, signs_ref,
    mix, chosen, scale, *rest,
):
    wide_refs, rest = rest[:len(CHUNK_REFS)], rest[len(CHUNK_REFS):]
    narrow_refs, rest = rest[:len(CHUNK_REFS)], rest[len(CHUNK_REFS):]
    small_sem, load_sem, send1, recv1, send2, recv2, send3, recv3, near = rest
    my_group = lax.axis_index("band")
    my_slab = lax.axis_index("gslab")
    my_core = lax.rem(my_group, 2)
    bits = (my_group // 4, lax.rem(my_group // 2, 2))
    per_slice, local_bands = signs_ref.shape
    slices = widths_ref.shape[0]
    packed = mix.shape[0]
    live = reach * per_slice
    peers = 4 * slabs
    mine = out_ref.shape[0]
    extra = mine - HALF
    tall_block = mine * slabs
    row_tiles = slabs - 1
    chunks = []
    start = 0
    for refs, tiles in ((wide_refs, 2), (narrow_refs, 1)):
        for place in range(refs[0].shape[0]):
            chunks.append(Chunk(len(chunks), place, start, tiles, refs))
            start += tiles * LANES
    quarter_columns = start
    count = len(chunks)

    def group_of(axis, along, other, core):
        return along * 4 + other * 2 + core if axis == 0 else other * 4 + along * 2 + core

    def own(axis):
        return bits[axis], bits[1 - axis]

    def here_at(axis):
        return own(axis)[0] * 2 + my_core

    def quarter_at(axis, k):
        return lax.rem(own(axis)[0] * 2 + 2 + k // 2 * 2, 4) + lax.rem(my_core + k + k // 2, 2)

    def load(chunk, quarter):
        start = quarter * quarter_columns + chunk.start
        return pltpu.make_async_copy(
            band_ref.at[:, pl.ds(pl.multiple_of(start, LANES), chunk.width)],
            chunk.held.at[quarter],
            load_sem.at[chunk.index % 3],
        )

    def load_chunk(chunk):
        for quarter in range(4):
            load(chunk, quarter).start()

    def wait_bytes(ref, semaphore):
        pltpu.make_async_copy(ref, ref, semaphore).wait()

    small = [
        pltpu.make_async_copy(signs_hbm, signs_ref, small_sem.at[0]),
        pltpu.make_async_copy(widths_hbm, widths_ref, small_sem.at[1]),
        pltpu.make_async_copy(owner_hbm, owner_ref, small_sem.at[2]),
    ]
    for copy in small:
        copy.start()
    load_chunk(chunks[0])

    barrier = pltpu.get_barrier_semaphore()

    def greet(semaphore, group, slab):
        pl.semaphore_signal(
            semaphore, inc=1, device_id={"band": group, "gslab": slab}, device_id_type=MESH
        )

    inner = lax.rem(my_slab + slabs - 1, slabs) // row_tiles
    outer = my_slab // row_tiles
    sides = 2 - inner - outer

    def greet_sides(semaphore):
        @pl.when(my_slab > 0)
        def _():
            greet(semaphore, my_group, my_slab - 1)

        @pl.when(my_slab < slabs - 1)
        def _():
            greet(semaphore, my_group, my_slab + 1)

    greet(barrier, group_of(0, bits[0], bits[1], 1 - my_core), my_slab)
    for axis in range(2):
        along, other = own(axis)
        for core in range(2):
            greet(barrier, group_of(axis, 1 - along, other, core), my_slab)
    greet_sides(barrier)
    load_chunk(chunks[1])
    for copy in small:
        copy.wait()

    ends = []
    running = jnp.int32(0)
    for s in range(slices):
        running = running + widths_ref[s]
        ends.append(running)

    first_band = my_group * local_bands
    bands = first_band + lax.broadcasted_iota(jnp.int32, (1, local_bands), 1)
    slice_of = jnp.zeros((1, local_bands), jnp.int32)
    first = jnp.int32(0)
    for s in range(slices):
        slice_of = slice_of + jnp.where(bands >= ends[s], 1, 0)
        first = first + jnp.where(first_band >= ends[s], 1, 0)
    row = lax.broadcasted_iota(jnp.int32, (packed, per_slice), 0)
    column = lax.broadcasted_iota(jnp.int32, (packed, per_slice), 1)
    repeat = jnp.where(lax.rem(row, per_slice) == column, 1.0, 0.0).astype(jnp.float32)
    signs = jnp.dot(
        repeat, signs_ref[...].astype(jnp.float32), preferred_element_type=jnp.float32
    )
    row = lax.broadcasted_iota(jnp.int32, (packed, local_bands), 0)
    hit = (slice_of - first == row // per_slice) & (row < live)
    mix[...] = jnp.where(hit, signs, 0.0).astype(jnp.bfloat16)

    def exchange(chunk, quarter, source):
        return pltpu.make_async_remote_copy(
            src_ref=chunk.sent.at[quarter],
            dst_ref=chunk.got.at[source],
            send_sem=send1,
            recv_sem=recv1.at[chunk.index],
            device_id={
                "band": group_of(chunk.axis, quarter // 2, own(chunk.axis)[1], lax.rem(quarter, 2)),
                "gslab": my_slab,
            },
            device_id_type=MESH,
        )

    def partial_sums(chunk, quarter):
        sums = two_term_dot(mix[...], chunk.held[quarter])
        return sums[:live].reshape(live // HALF, HALF, chunk.width)

    def ready(chunk):
        if chunk.index + 2 < count:
            load_chunk(chunks[chunk.index + 2])
        wait_bytes(chunk.held, load_sem.at[chunk.index % 3])

    def send_partial(chunk, first=0, last=4):
        here = here_at(chunk.axis)

        @pl.loop(first, min(last, 3))
        def _(k):
            quarter = quarter_at(chunk.axis, k)
            chunk.sent[quarter] = partial_sums(chunk, quarter)
            exchange(chunk, quarter, here).start()

        if last == 4:
            chunk.got[here] = partial_sums(chunk, here)

    def cross(chunk):
        along, other = own(chunk.axis)
        return pltpu.make_async_remote_copy(
            src_ref=chunk.half.at[0],
            dst_ref=chunk.came,
            send_sem=send2,
            recv_sem=recv2.at[chunk.index],
            device_id={"band": group_of(chunk.axis, along, 1 - other, my_core), "gslab": my_slab},
            device_id_type=MESH,
        )

    def merge(chunk):
        wait_bytes(chunk.got.at[pl.ds(0, 3)], recv1.at[chunk.index])
        rows = chunk.got[...].reshape(4 * live, chunk.width)
        value = two_term_dot(chosen[chunk.axis], rows)
        chunk.half[...] = value.reshape(2, peers * mine, chunk.width)
        cross(chunk).start()

    def deliver(chunk, slab, quarter):
        return pltpu.make_async_remote_copy(
            src_ref=chunk.done.at[quarter * slabs + slab],
            dst_ref=chunk.parcel.at[my_slab, here_at(chunk.axis)],
            send_sem=send3,
            recv_sem=recv3.at[chunk.index],
            device_id={
                "band": group_of(chunk.axis, quarter // 2, own(chunk.axis)[1], lax.rem(quarter, 2)),
                "gslab": slab,
            },
            device_id_type=MESH,
        )

    def finish(chunk):
        here = here_at(chunk.axis)
        cross(chunk).wait_recv()
        total = (chunk.half[1] + chunk.came[...]) * scale[chunk.axis, :, :1]
        total = total.reshape(4 * row_tiles, SUBLANES, chunk.width)
        level = lax.broadcasted_iota(jnp.int32, (SUBLANES, LANES), 0)
        early = level % HALF < extra
        for peer in range(peers if chunk.tiles == 1 else 0):
            quarter, slab = divmod(peer, slabs)
            tile = [total[quarter * row_tiles + k] for k in range(row_tiles)]
            for at in range(0, HALF, extra):
                place = slab % 2 * HALF + at
                chunk.done[peer, at // extra] = tile[slab // 2][place:place + extra]
            chunk.done[peer, HALF // extra] = tile[-1][slab * extra:(slab + 1) * extra]
        for quarter in range(4 if chunk.tiles == 2 else 0):
            tile = [total[quarter * row_tiles + k] for k in range(row_tiles)]
            left = [t[:, :LANES] for t in tile]
            right = [t[:, LANES:] for t in tile]
            even = jnp.where(early, left[-1], pltpu.roll(right[-1], extra, 0))
            odd = jnp.where(early, pltpu.roll(left[-1], SUBLANES - extra, 0), right[-1])
            for slab in range(slabs):
                at = slab % 2 * HALF
                end = slab // 2 * HALF
                peer = quarter * slabs + slab
                chunk.done[peer, 0] = left[slab // 2][at:at + HALF]
                chunk.done[peer, 1] = right[slab // 2][at:at + HALF]
                chunk.done[peer, 2] = (odd if slab % 2 else even)[end:end + HALF]
        pltpu.make_async_copy(
            chunk.done.at[here * slabs + my_slab],
            chunk.parcel.at[my_slab, here],
            recv3.at[chunk.index],
        ).start()
        side = my_slab // 2

        @pl.loop(0, 8)
        def _(k):
            deliver(chunk, 2 - 2 * side + k // 4, lax.rem(here + k, 4)).start()

        @pl.loop(0, 4)
        def _(k):
            deliver(chunk, 4 * side + 1 - my_slab, lax.rem(here + k, 4)).start()

        @pl.loop(1, 4)
        def _(k):
            deliver(chunk, my_slab, lax.rem(here + k, 4)).start()

    def unpack(chunk):
        wait_bytes(chunk.parcel, recv3.at[chunk.index])
        for slab in range(slabs):
            for quarter in range(4):
                at = (slab * 4 + quarter) * quarter_columns + chunk.start
                if chunk.tiles == 1:
                    columns = slice(at, at + LANES)
                    for piece in range(mine // extra):
                        rows = slice(piece * extra, (piece + 1) * extra)
                        out_ref[rows, columns] = chunk.parcel[slab, quarter, piece]
                    continue
                for tile in range(2):
                    columns = slice(at + tile * LANES, at + (tile + 1) * LANES)
                    out_ref[:HALF, columns] = chunk.parcel[slab, quarter, tile]
                    out_ref[HALF:, columns] = chunk.parcel[
                        slab, quarter, 2, tile * extra:(tile + 1) * extra
                    ]

    lead, second = chunks[:2]
    ready(lead)

    @pl.loop(0, 2)
    def _(k):
        quarter = quarter_at(0, k)
        lead.sent[quarter] = partial_sums(lead, quarter)

    pl.semaphore_wait(barrier, 5 + sides)

    @pl.loop(0, 2)
    def _(k):
        exchange(lead, quarter_at(0, k), here_at(0)).start()

    ready(second)
    send_partial(second, 0, 2)
    send_partial(lead, 2, 4)
    send_partial(second, 2, 4)
    greet_sides(near.at[0])

    for axis in range(2):
        along, other = own(axis)
        shape = (2 * peers * mine, 1)
        tall = lax.broadcasted_iota(jnp.int32, shape, 0)
        stays = tall // (peers * mine)
        rest = lax.rem(tall, peers * mine)
        quarter = rest // tall_block
        rest = lax.rem(rest, tall_block)
        low = rest < slabs * HALF
        beyond = rest - slabs * HALF
        slab = jnp.where(low, rest // HALF, beyond // extra)
        within = jnp.where(low, lax.rem(rest, HALF), HALF + lax.rem(beyond, extra))
        side = jnp.where(stays == 1, other, 1 - other)
        group = group_of(axis, quarter // 2, side, lax.rem(quarter, 2))
        output_row = (group * slabs + slab) * mine + within
        block = output_row // per_slice
        target = jnp.zeros(shape, jnp.int32)
        for s in range(slices):
            target = jnp.where(block == s, owner_ref[s], target)
        breadth = jnp.ones(shape, jnp.int32)
        for s in range(slices):
            breadth = jnp.where(target == s, widths_ref[s], breadth)
        root = 1.0 / jnp.sqrt(breadth.astype(jnp.float32))
        scale[axis] = jnp.broadcast_to(root[peers * mine:], (peers * mine, LANES))
        wanted = target * per_slice + lax.rem(output_row, per_slice)
        wide = lax.broadcasted_iota(jnp.int32, (1, 4 * live), 1)
        place = lax.rem(wide, live)
        quarter = wide // live
        begin = group_of(axis, quarter // 2, other, lax.rem(quarter, 2)) * local_bands
        lowest = jnp.zeros((1, 4 * live), jnp.int32)
        for s in range(slices):
            lowest = lowest + jnp.where(begin >= ends[s], 1, 0)
        offered = lowest * per_slice + place
        chosen[axis] = jnp.where(wanted == offered, 1.0, 0.0).astype(jnp.bfloat16)

    known = 0

    def learn():
        pl.semaphore_wait(near.at[known], sides)
        if known + 1 < row_tiles:
            greet_sides(near.at[known + 1])

    for step in range(2, count + UNPACK_LAG):
        if step < count:
            ready(chunks[step])
            send_partial(chunks[step])
        if known < row_tiles:
            learn()
            known += 1
        if 0 <= step - MERGE_LAG < count:
            merge(chunks[step - MERGE_LAG])
        if 0 <= step - FINISH_LAG < count:
            finish(chunks[step - FINISH_LAG])
        if 0 <= step - UNPACK_LAG < count:
            unpack(chunks[step - UNPACK_LAG])

    for refs in (wide_refs, narrow_refs):
        named = dict(zip(CHUNK_REFS, refs))
        wait_bytes(named["sent"].at[:, pl.ds(0, 3)], send1)
        wait_bytes(named["came"], send2)
        wait_bytes(named["done"].at[:, pl.ds(0, peers - 1)], send3)


def on_device(groups, slabs, band_coeffs, sign_table, slice_widths, owner_map):
    local_bands, local_columns = band_coeffs.shape
    per_slice = sign_table.shape[0]
    rows = owner_map.shape[0] * per_slice
    tiles, odd = divmod(local_columns, 4 * LANES)
    mine = rows // (8 * slabs)
    reach = (local_bands - 2) // NARROWEST + 2
    live = reach * per_slice
    fits = 2 * (mine - HALF) == HALF and slabs == HALF and live % HALF == 0
    if groups != 8 or odd or rows % (8 * slabs) or not fits or tiles % 2 or tiles <= NARROW:
        return dense(band_coeffs, sign_table, slice_widths, owner_map)
    peers = 4 * slabs
    extra = mine - HALF

    def buffers(count, tiles):
        width = tiles * LANES
        block = (mine * tiles // HALF, HALF, LANES) if tiles == 2 else (mine // extra, extra, LANES)
        return [
            pltpu.VMEM((count, 4, local_bands, width), jnp.float32),
            pltpu.VMEM((count, 4, live // HALF, HALF, width), jnp.float32),
            pltpu.VMEM((count, 4, live // HALF, HALF, width), jnp.float32),
            pltpu.VMEM((count, 2, peers * mine, width), jnp.float32),
            pltpu.VMEM((count, peers * mine, width), jnp.float32),
            pltpu.VMEM((count, peers, *block), jnp.float32),
            pltpu.VMEM((count, slabs, 4, *block), jnp.float32),
        ]

    wide = (tiles - NARROW) // 2
    count = wide + NARROW
    return pl.pallas_call(
        functools.partial(kernel, slabs, reach),
        out_shape=pltpu.VMEM((mine, local_columns * slabs), jnp.float32),
        in_specs=[pl.BlockSpec(memory_space=pl.ANY)] * 4,
        out_specs=pl.BlockSpec(memory_space=pltpu.VMEM),
        scratch_shapes=[
            pltpu.SMEM(slice_widths.shape, jnp.int32),
            pltpu.SMEM(owner_map.shape, jnp.int32),
            pltpu.VMEM(sign_table.shape, jnp.int32),
            pltpu.VMEM((-(-live // SUBLANES) * SUBLANES, local_bands), jnp.bfloat16),
            pltpu.VMEM((2, 2 * peers * mine, 4 * live), jnp.bfloat16),
            pltpu.VMEM((2, peers * mine, LANES), jnp.float32),
            *buffers(wide, 2),
            *buffers(NARROW, 1),
            pltpu.SemaphoreType.DMA((3,)),
            pltpu.SemaphoreType.DMA((3,)),
            pltpu.SemaphoreType.DMA,
            pltpu.SemaphoreType.DMA((count,)),
            pltpu.SemaphoreType.DMA,
            pltpu.SemaphoreType.DMA((count,)),
            pltpu.SemaphoreType.DMA,
            pltpu.SemaphoreType.DMA((count,)),
            pltpu.SemaphoreType.REGULAR((slabs - 1,)),
        ],
        compiler_params=pltpu.CompilerParams(
            collective_id=0,
            has_side_effects=True,
            vmem_limit_bytes=VMEM - SUBLANES * local_columns * slabs * 4,
        ),
        name="pseudobands",
    )(slice_widths, owner_map, sign_table, band_coeffs)


def solution(mesh):
    return jax.shard_map(
        functools.partial(on_device, mesh.shape["band"], mesh.shape["gslab"]),
        mesh=mesh,
        in_specs=(P("band", "gslab"), P(None, "band"), P(), P()),
        out_specs=P(("band", "gslab"), None),
        check_vma=False,
    )
```

time: 52.5 us -> 50.1 us (0.954)
  Pallas kernels: 51.2 us -> 48.8 us
    pallas_call x1, Pallas kernels: 51.2 us -> 48.8 us  [on_device(): pl.pallas_call(functools.partial(kernel, slabs, reach), out_shape=pltpu.V...]
where the time goes in v2:
time: 50.1 us; the launch traced here: 50 us
  Pallas kernels  48.8 us (97%)
  local copies, waits for them, and re-layouts  1.15 us (2%)
    pallas_call x1, Pallas kernels, on_device(): pl.pallas_call(functools.partial(kernel, slabs, reach), out_shape=pltpu.V...  48.8 us
    unnamed x1, local copies, waits for them, and re-layouts  1.15 us

profile of v2, /device:TPU:0, one launch (start us, length us, event | category | flops | bytes accessed | tf_op | source)
XLA Modules:
  0.0 50.0 jit_solution(8383753720431603421)
XLA Ops:
  0.0 48.8 %pseudobands.1 = f32[6,49152]{1,0:T(8,128)S(1)} custom-call(s32[16]{0:T(128)} %widths_hbm.1, s32[16]{0:T(128)} %owner_hbm.1, s32[12,384]{1,0:T(8,128)} %signs_hbm.1, f32[384,12288]{1,0:T(8,128)} %band_ref.1), custom_call_target="tpu_custom_call" | custom-call | tf_op jit(solution)/shard_map/pseudobands/pallas_call | solution.py:442
  48.8 1.1 %copy.6 = f32[6,49152]{1,0:T(8,128)} copy(f32[6,49152]{1,0:T(8,128)S(1)} %pseudobands.1) | data formatting | bytes 2359296

commit v3 on v2

--- a/solution.py
+++ b/solution.py
@@ -12,11 +12,15 @@
 SUBLANES = 8
 HALF = 4
 VMEM = 67043328
-CHUNK_REFS = ("held", "sent", "got", "half", "came", "done", "parcel")
+COMMON_REFS = ("held", "half", "came", "done", "parcel", "sent", "got")
+LEAD = 2
+CHUNK_REFS = (COMMON_REFS, *[COMMON_REFS + ("keep", "give", "take")] * 2)
 NARROW = 2
 MERGE_LAG = 2
-FINISH_LAG = 4
-UNPACK_LAG = 7
+NEAR_LAG = 3
+FAR_LAG = 4
+FINISH_LAG = 6
+UNPACK_LAG = 8
 MESH = pl.DeviceIdType.MESH
 
 
@@ -71,30 +75,31 @@
 
 
 class Chunk:
-    def __init__(self, index, place, start, tiles, refs):
+    def __init__(self, index, place, start, tiles, names, refs):
         self.index, self.axis, self.start, self.tiles = index, index % 2, start, tiles
         self.width = tiles * LANES
-        for name, ref in zip(CHUNK_REFS, refs):
+        for name, ref in zip(names, refs):
             setattr(self, name, ref.at[place])
 
 
 def kernel(
-    slabs, reach,
+    slabs, reach, chip_reach,
     widths_hbm, owner_hbm, signs_hbm, band_ref, out_ref,
     widths_ref, owner_ref, signs_ref,
-    mix, chosen, scale, *rest,
+    mix, chip_mix, chosen, chip_chosen, scale, *rest,
 ):
-    wide_refs, rest = rest[:len(CHUNK_REFS)], rest[len(CHUNK_REFS):]
-    narrow_refs, rest = rest[:len(CHUNK_REFS)], rest[len(CHUNK_REFS):]
-    small_sem, load_sem, send1, recv1, send2, recv2, send3, recv3, near = rest
+    groups = []
+    for names in CHUNK_REFS:
+        groups.append(rest[:len(names)])
+        rest = rest[len(names):]
+    small_sem, load_sem, send1, recv1, send2, recv2, send3, recv3, pair_sem, near = rest
     my_group = lax.axis_index("band")
     my_slab = lax.axis_index("gslab")
     my_core = lax.rem(my_group, 2)
     bits = (my_group // 4, lax.rem(my_group // 2, 2))
     per_slice, local_bands = signs_ref.shape
     slices = widths_ref.shape[0]
-    packed = mix.shape[0]
-    live = reach * per_slice
+    live, chip_live = reach * per_slice, chip_reach * per_slice
     peers = 4 * slabs
     mine = out_ref.shape[0]
     extra = mine - HALF
@@ -102,9 +107,9 @@
     row_tiles = slabs - 1
     chunks = []
     start = 0
-    for refs, tiles in ((wide_refs, 2), (narrow_refs, 1)):
+    for names, refs, tiles in zip(CHUNK_REFS, groups, (2, 2, 1)):
         for place in range(refs[0].shape[0]):
-            chunks.append(Chunk(len(chunks), place, start, tiles, refs))
+            chunks.append(Chunk(len(chunks), place, start, tiles, names, refs))
             start += tiles * LANES
     quarter_columns = start
     count = len(chunks)
@@ -184,19 +189,25 @@
     first_band = my_group * local_bands
     bands = first_band + lax.broadcasted_iota(jnp.int32, (1, local_bands), 1)
     slice_of = jnp.zeros((1, local_bands), jnp.int32)
-    first = jnp.int32(0)
     for s in range(slices):
         slice_of = slice_of + jnp.where(bands >= ends[s], 1, 0)
-        first = first + jnp.where(first_band >= ends[s], 1, 0)
-    row = lax.broadcasted_iota(jnp.int32, (packed, per_slice), 0)
-    column = lax.broadcasted_iota(jnp.int32, (packed, per_slice), 1)
-    repeat = jnp.where(lax.rem(row, per_slice) == column, 1.0, 0.0).astype(jnp.float32)
-    signs = jnp.dot(
-        repeat, signs_ref[...].astype(jnp.float32), preferred_element_type=jnp.float32
-    )
-    row = lax.broadcasted_iota(jnp.int32, (packed, local_bands), 0)
-    hit = (slice_of - first == row // per_slice) & (row < live)
-    mix[...] = jnp.where(hit, signs, 0.0).astype(jnp.bfloat16)
+
+    def fill(target, band, extent):
+        first = jnp.int32(0)
+        for s in range(slices):
+            first = first + jnp.where(band >= ends[s], 1, 0)
+        packed = target.shape[0]
+        row = lax.broadcasted_iota(jnp.int32, (packed, per_slice), 0)
+        column = lax.broadcasted_iota(jnp.int32, (packed, per_slice), 1)
+        repeat = jnp.where(lax.rem(row, per_slice) == column, 1.0, 0.0).astype(jnp.float32)
+        signs = jnp.dot(
+            repeat, signs_ref[...].astype(jnp.float32), preferred_element_type=jnp.float32
+        )
+        row = lax.broadcasted_iota(jnp.int32, (packed, local_bands), 0)
+        hit = (slice_of - first == row // per_slice) & (row < extent)
+        target[...] = jnp.where(hit, signs, 0.0).astype(jnp.bfloat16)
+
+    fill(mix, first_band, live)
 
     def exchange(chunk, quarter, source):
         return pltpu.make_async_remote_copy(
@@ -215,6 +226,51 @@
         sums = two_term_dot(mix[...], chunk.held[quarter])
         return sums[:live].reshape(live // HALF, HALF, chunk.width)
 
+    def chip_sums(chunk, quarter):
+        sums = two_term_dot(chip_mix[...], chunk.held[quarter])
+        return sums[:chip_live].reshape(chip_live // HALF, HALF, chunk.width)
+
+    def pair(chunk, k):
+        return pltpu.make_async_remote_copy(
+            src_ref=chunk.give.at[k],
+            dst_ref=chunk.take.at[k],
+            send_sem=send1,
+            recv_sem=pair_sem.at[chunk.index - LEAD],
+            device_id={"band": my_group + 1 - 2 * my_core, "gslab": my_slab},
+            device_id_type=MESH,
+        )
+
+    def pair_partial(chunk):
+        along = own(chunk.axis)[0]
+
+        @pl.loop(0, 2)
+        def _(k):
+            side = lax.rem(along + 1 + k, 2)
+            chunk.give[k] = chip_sums(chunk, side * 2 + 1 - my_core)
+            pair(chunk, k).start()
+
+        @pl.loop(0, 2)
+        def _(k):
+            side = lax.rem(along + 1 + k, 2)
+            chunk.keep[k] = chip_sums(chunk, side * 2 + my_core)
+
+    def across(chunk):
+        along, other = own(chunk.axis)
+        return pltpu.make_async_remote_copy(
+            src_ref=chunk.sent,
+            dst_ref=chunk.got.at[along],
+            send_sem=send1,
+            recv_sem=recv1.at[chunk.index],
+            device_id={"band": group_of(chunk.axis, 1 - along, other, my_core), "gslab": my_slab},
+            device_id_type=MESH,
+        )
+
+    def fold(chunk):
+        wait_bytes(chunk.take, pair_sem.at[chunk.index - LEAD])
+        chunk.sent[...] = chunk.keep[0] + chunk.take[0]
+        across(chunk).start()
+        chunk.got[own(chunk.axis)[0]] = chunk.keep[1] + chunk.take[1]
+
     def ready(chunk):
         if chunk.index + 2 < count:
             load_chunk(chunks[chunk.index + 2])
@@ -232,82 +288,93 @@
         if last == 4:
             chunk.got[here] = partial_sums(chunk, here)
 
-    def cross(chunk):
+    def side_of(far):
+        return 1 - my_slab // 2 if far else my_slab // 2
+
+    def rows_of(far):
+        return pl.ds(pl.multiple_of(side_of(far) * (2 * tall_block), SUBLANES), 2 * tall_block)
+
+    def cross(chunk, far):
         along, other = own(chunk.axis)
         return pltpu.make_async_remote_copy(
-            src_ref=chunk.half.at[0],
-            dst_ref=chunk.came,
+            src_ref=chunk.half.at[0, rows_of(far)],
+            dst_ref=chunk.came.at[rows_of(far)],
             send_sem=send2,
-            recv_sem=recv2.at[chunk.index],
+            recv_sem=recv2.at[2 * chunk.index + far],
             device_id={"band": group_of(chunk.axis, along, 1 - other, my_core), "gslab": my_slab},
             device_id_type=MESH,
         )
 
     def merge(chunk):
-        wait_bytes(chunk.got.at[pl.ds(0, 3)], recv1.at[chunk.index])
-        rows = chunk.got[...].reshape(4 * live, chunk.width)
-        value = two_term_dot(chosen[chunk.axis], rows)
+        if chunk.index < LEAD:
+            wait_bytes(chunk.got.at[pl.ds(0, 3)], recv1.at[chunk.index])
+            rows = chunk.got[...].reshape(4 * live, chunk.width)
+            value = two_term_dot(chosen[chunk.axis], rows)
+        else:
+            wait_bytes(chunk.got.at[0], recv1.at[chunk.index])
+            rows = chunk.got[...].reshape(2 * chip_live, chunk.width)
+            value = two_term_dot(chip_chosen[chunk.axis], rows)
         chunk.half[...] = value.reshape(2, peers * mine, chunk.width)
-        cross(chunk).start()
-
-    def deliver(chunk, slab, quarter):
+        cross(chunk, 1).start()
+
+    def deliver(chunk, far, place):
+        side = side_of(far)
+        quarter = place // 2
         return pltpu.make_async_remote_copy(
-            src_ref=chunk.done.at[quarter * slabs + slab],
+            src_ref=chunk.done.at[side * (peers // 2) + place],
             dst_ref=chunk.parcel.at[my_slab, here_at(chunk.axis)],
             send_sem=send3,
             recv_sem=recv3.at[chunk.index],
             device_id={
                 "band": group_of(chunk.axis, quarter // 2, own(chunk.axis)[1], lax.rem(quarter, 2)),
-                "gslab": slab,
+                "gslab": 2 * side + lax.rem(place, 2),
             },
             device_id_type=MESH,
         )
 
-    def finish(chunk):
+    def finish(chunk, far):
         here = here_at(chunk.axis)
-        cross(chunk).wait_recv()
-        total = (chunk.half[1] + chunk.came[...]) * scale[chunk.axis, :, :1]
-        total = total.reshape(4 * row_tiles, SUBLANES, chunk.width)
+        cross(chunk, far).wait_recv()
+        rows = rows_of(far)
+        total = (chunk.half[1, rows] + chunk.came[rows]) * scale[chunk.axis, rows, :1]
+        total = total.reshape(2 * row_tiles, SUBLANES, chunk.width)
         level = lax.broadcasted_iota(jnp.int32, (SUBLANES, LANES), 0)
         early = level % HALF < extra
-        for peer in range(peers if chunk.tiles == 1 else 0):
-            quarter, slab = divmod(peer, slabs)
-            tile = [total[quarter * row_tiles + k] for k in range(row_tiles)]
-            for at in range(0, HALF, extra):
-                place = slab % 2 * HALF + at
-                chunk.done[peer, at // extra] = tile[slab // 2][place:place + extra]
-            chunk.done[peer, HALF // extra] = tile[-1][slab * extra:(slab + 1) * extra]
-        for quarter in range(4 if chunk.tiles == 2 else 0):
-            tile = [total[quarter * row_tiles + k] for k in range(row_tiles)]
+        first = side_of(far) * (peers // 2)
+        for group in range(2):
+            tile = [total[group * row_tiles + k] for k in range(row_tiles)]
+            if chunk.tiles == 1:
+                for place in range(slabs):
+                    peer = first + group * slabs + place
+                    for at in range(0, HALF, extra):
+                        row = place % 2 * HALF + at
+                        chunk.done[peer, at // extra] = tile[place // 2][row:row + extra]
+                    chunk.done[peer, HALF // extra] = tile[-1][place * extra:(place + 1) * extra]
+                continue
             left = [t[:, :LANES] for t in tile]
             right = [t[:, LANES:] for t in tile]
             even = jnp.where(early, left[-1], pltpu.roll(right[-1], extra, 0))
             odd = jnp.where(early, pltpu.roll(left[-1], SUBLANES - extra, 0), right[-1])
-            for slab in range(slabs):
-                at = slab % 2 * HALF
-                end = slab // 2 * HALF
-                peer = quarter * slabs + slab
-                chunk.done[peer, 0] = left[slab // 2][at:at + HALF]
-                chunk.done[peer, 1] = right[slab // 2][at:at + HALF]
-                chunk.done[peer, 2] = (odd if slab % 2 else even)[end:end + HALF]
-        pltpu.make_async_copy(
-            chunk.done.at[here * slabs + my_slab],
-            chunk.parcel.at[my_slab, here],
-            recv3.at[chunk.index],
-        ).start()
-        side = my_slab // 2
-
-        @pl.loop(0, 8)
-        def _(k):
-            deliver(chunk, 2 - 2 * side + k // 4, lax.rem(here + k, 4)).start()
-
-        @pl.loop(0, 4)
-        def _(k):
-            deliver(chunk, 4 * side + 1 - my_slab, lax.rem(here + k, 4)).start()
-
-        @pl.loop(1, 4)
-        def _(k):
-            deliver(chunk, my_slab, lax.rem(here + k, 4)).start()
+            for place in range(slabs):
+                at = place % 2 * HALF
+                end = place // 2 * HALF
+                peer = first + group * slabs + place
+                chunk.done[peer, 0] = left[place // 2][at:at + HALF]
+                chunk.done[peer, 1] = right[place // 2][at:at + HALF]
+                chunk.done[peer, 2] = (odd if place % 2 else even)[end:end + HALF]
+        myself = here * 2 + lax.rem(my_slab, 2)
+        if far:
+            @pl.loop(0, 8)
+            def _(k):
+                deliver(chunk, 1, lax.rem(myself + k, 8)).start()
+        else:
+            pltpu.make_async_copy(
+                chunk.done.at[first + myself], chunk.parcel.at[my_slab, here], recv3.at[chunk.index]
+            ).start()
+
+            @pl.loop(1, 8)
+            def _(k):
+                deliver(chunk, 0, lax.rem(myself + k, 8)).start()
 
     def unpack(chunk):
         wait_bytes(chunk.parcel, recv3.at[chunk.index])
@@ -346,6 +413,9 @@
     send_partial(lead, 2, 4)
     send_partial(second, 2, 4)
     greet_sides(near.at[0])
+    fill(chip_mix, (my_group - my_core) * local_bands, chip_live)
+    ready(chunks[LEAD])
+    pair_partial(chunks[LEAD])
 
     for axis in range(2):
         along, other = own(axis)
@@ -353,11 +423,13 @@
         tall = lax.broadcasted_iota(jnp.int32, shape, 0)
         stays = tall // (peers * mine)
         rest = lax.rem(tall, peers * mine)
-        quarter = rest // tall_block
+        part = rest // tall_block
         rest = lax.rem(rest, tall_block)
         low = rest < slabs * HALF
         beyond = rest - slabs * HALF
-        slab = jnp.where(low, rest // HALF, beyond // extra)
+        place = jnp.where(low, rest // HALF, beyond // extra)
+        quarter = lax.rem(part, 2) * 2 + place // 2
+        slab = part // 2 * 2 + lax.rem(place, 2)
         within = jnp.where(low, lax.rem(rest, HALF), HALF + lax.rem(beyond, extra))
         side = jnp.where(stays == 1, other, 1 - other)
         group = group_of(axis, quarter // 2, side, lax.rem(quarter, 2))
@@ -372,15 +444,16 @@
         root = 1.0 / jnp.sqrt(breadth.astype(jnp.float32))
         scale[axis] = jnp.broadcast_to(root[peers * mine:], (peers * mine, LANES))
         wanted = target * per_slice + lax.rem(output_row, per_slice)
-        wide = lax.broadcasted_iota(jnp.int32, (1, 4 * live), 1)
-        place = lax.rem(wide, live)
-        quarter = wide // live
-        begin = group_of(axis, quarter // 2, other, lax.rem(quarter, 2)) * local_bands
-        lowest = jnp.zeros((1, 4 * live), jnp.int32)
-        for s in range(slices):
-            lowest = lowest + jnp.where(begin >= ends[s], 1, 0)
-        offered = lowest * per_slice + place
-        chosen[axis] = jnp.where(wanted == offered, 1.0, 0.0).astype(jnp.bfloat16)
+        for target, cores, extent in ((chosen, 2, live), (chip_chosen, 1, chip_live)):
+            wide = lax.broadcasted_iota(jnp.int32, (1, 2 * cores * extent), 1)
+            place = lax.rem(wide, extent)
+            source = wide // extent
+            begin = group_of(axis, source // cores, other, lax.rem(source, cores)) * local_bands
+            lowest = jnp.zeros(wide.shape, jnp.int32)
+            for s in range(slices):
+                lowest = lowest + jnp.where(begin >= ends[s], 1, 0)
+            offered = lowest * per_slice + place
+            target[axis] = jnp.where(wanted == offered, 1.0, 0.0).astype(jnp.bfloat16)
 
     known = 0
 
@@ -389,23 +462,33 @@
         if known + 1 < row_tiles:
             greet_sides(near.at[known + 1])
 
-    for step in range(2, count + UNPACK_LAG):
+    for step in range(LEAD, count + UNPACK_LAG):
         if step < count:
-            ready(chunks[step])
-            send_partial(chunks[step])
+            fold(chunks[step])
+        if step + 1 < count:
+            ready(chunks[step + 1])
+            pair_partial(chunks[step + 1])
         if known < row_tiles:
             learn()
             known += 1
         if 0 <= step - MERGE_LAG < count:
             merge(chunks[step - MERGE_LAG])
+        if 0 <= step - NEAR_LAG < count:
+            cross(chunks[step - NEAR_LAG], 0).start()
+        if 0 <= step - FAR_LAG < count:
+            finish(chunks[step - FAR_LAG], 1)
         if 0 <= step - FINISH_LAG < count:
-            finish(chunks[step - FINISH_LAG])
+            finish(chunks[step - FINISH_LAG], 0)
         if 0 <= step - UNPACK_LAG < count:
             unpack(chunks[step - UNPACK_LAG])
 
-    for refs in (wide_refs, narrow_refs):
-        named = dict(zip(CHUNK_REFS, refs))
-        wait_bytes(named["sent"].at[:, pl.ds(0, 3)], send1)
+    for names, refs in zip(CHUNK_REFS, groups):
+        named = dict(zip(names, refs))
+        if "give" in named:
+            wait_bytes(named["give"], send1)
+            wait_bytes(named["sent"], send1)
+        else:
+            wait_bytes(named["sent"].at[:, pl.ds(0, 3)], send1)
         wait_bytes(named["came"], send2)
         wait_bytes(named["done"].at[:, pl.ds(0, peers - 1)], send3)
 
@@ -417,30 +500,35 @@
     tiles, odd = divmod(local_columns, 4 * LANES)
     mine = rows // (8 * slabs)
     reach = (local_bands - 2) // NARROWEST + 2
-    live = reach * per_slice
-    fits = 2 * (mine - HALF) == HALF and slabs == HALF and live % HALF == 0
-    if groups != 8 or odd or rows % (8 * slabs) or not fits or tiles % 2 or tiles <= NARROW:
+    chip_reach = (2 * local_bands - 2) // NARROWEST + 2
+    live, chip_live = reach * per_slice, chip_reach * per_slice
+    fits = 2 * (mine - HALF) == HALF and slabs == HALF and per_slice % HALF == 0
+    if groups != 8 or odd or rows % (8 * slabs) or not fits or tiles % 2 or tiles <= NARROW + 2 * LEAD:
         return dense(band_coeffs, sign_table, slice_widths, owner_map)
     peers = 4 * slabs
     extra = mine - HALF
 
-    def buffers(count, tiles):
+    def buffers(count, tiles, paired):
         width = tiles * LANES
         block = (mine * tiles // HALF, HALF, LANES) if tiles == 2 else (mine // extra, extra, LANES)
-        return [
-            pltpu.VMEM((count, 4, local_bands, width), jnp.float32),
-            pltpu.VMEM((count, 4, live // HALF, HALF, width), jnp.float32),
-            pltpu.VMEM((count, 4, live // HALF, HALF, width), jnp.float32),
-            pltpu.VMEM((count, 2, peers * mine, width), jnp.float32),
-            pltpu.VMEM((count, peers * mine, width), jnp.float32),
-            pltpu.VMEM((count, peers, *block), jnp.float32),
-            pltpu.VMEM((count, slabs, 4, *block), jnp.float32),
+        core, chip = [(rows // HALF, HALF, width) for rows in (live, chip_live)]
+        shapes = [
+            (4, local_bands, width),
+            (2, peers * mine, width),
+            (peers * mine, width),
+            (peers, *block),
+            (slabs, 4, *block),
         ]
-
-    wide = (tiles - NARROW) // 2
-    count = wide + NARROW
+        shapes += [chip, *[(2, *chip)] * 4] if paired else [(4, *core)] * 2
+        return [pltpu.VMEM((count, *shape), jnp.float32) for shape in shapes]
+
+    def aligned(rows):
+        return -(-rows // SUBLANES) * SUBLANES
+
+    wide = (tiles - NARROW) // 2 - LEAD
+    count = LEAD + wide + NARROW
     return pl.pallas_call(
-        functools.partial(kernel, slabs, reach),
+        functools.partial(kernel, slabs, reach, chip_reach),
         out_shape=pltpu.VMEM((mine, local_columns * slabs), jnp.float32),
         in_specs=[pl.BlockSpec(memory_space=pl.ANY)] * 4,
         out_specs=pl.BlockSpec(memory_space=pltpu.VMEM),
@@ -448,19 +536,23 @@
             pltpu.SMEM(slice_widths.shape, jnp.int32),
             pltpu.SMEM(owner_map.shape, jnp.int32),
             pltpu.VMEM(sign_table.shape, jnp.int32),
-            pltpu.VMEM((-(-live // SUBLANES) * SUBLANES, local_bands), jnp.bfloat16),
+            pltpu.VMEM((aligned(live), local_bands), jnp.bfloat16),
+            pltpu.VMEM((aligned(chip_live), local_bands), jnp.bfloat16),
             pltpu.VMEM((2, 2 * peers * mine, 4 * live), jnp.bfloat16),
+            pltpu.VMEM((2, 2 * peers * mine, 2 * chip_live), jnp.bfloat16),
             pltpu.VMEM((2, peers * mine, LANES), jnp.float32),
-            *buffers(wide, 2),
-            *buffers(NARROW, 1),
+            *buffers(LEAD, 2, False),
+            *buffers(wide, 2, True),
+            *buffers(NARROW, 1, True),
             pltpu.SemaphoreType.DMA((3,)),
             pltpu.SemaphoreType.DMA((3,)),
             pltpu.SemaphoreType.DMA,
             pltpu.SemaphoreType.DMA((count,)),
             pltpu.SemaphoreType.DMA,
-            pltpu.SemaphoreType.DMA((count,)),
+            pltpu.SemaphoreType.DMA((2 * count,)),
             pltpu.SemaphoreType.DMA,
             pltpu.SemaphoreType.DMA((count,)),
+            pltpu.SemaphoreType.DMA((count - LEAD,)),
             pltpu.SemaphoreType.REGULAR((slabs - 1,)),
         ],
         compiler_params=pltpu.CompilerParams(

time: 50.1 us -> 48.1 us (0.960)
  Pallas kernels: 48.8 us -> 46.8 us
    pallas_call x1, Pallas kernels: 48.8 us -> 46.8 us  [on_device(): pl.pallas_call(functools.partial(kernel, slabs, reach, chip_reach), out_s...]
where the time goes in v3:
time: 48.1 us; the launch traced here: 48 us
  Pallas kernels  46.8 us (97%)
  local copies, waits for them, and re-layouts  1.15 us (2%)
    pallas_call x1, Pallas kernels, on_device(): pl.pallas_call(functools.partial(kernel, slabs, reach, chip_reach), out_s...  46.8 us
    unnamed x1, local copies, waits for them, and re-layouts  1.15 us

profile of v3, /device:TPU:0, one launch (start us, length us, event | category | flops | bytes accessed | tf_op | source)
XLA Modules:
  0.0 48.0 jit_solution(1607795362808257806)
XLA Ops:
  0.0 46.8 %pseudobands.1 = f32[6,49152]{1,0:T(8,128)S(1)} custom-call(s32[16]{0:T(128)} %widths_hbm.1, s32[16]{0:T(128)} %owner_hbm.1, s32[12,384]{1,0:T(8,128)} %signs_hbm.1, f32[384,12288]{1,0:T(8,128)} %band_ref.1), custom_call_target="tpu_custom_call" | custom-call | tf_op jit(solution)/shard_map/pseudobands/pallas_call | solution.py:530
  46.8 1.1 %copy.6 = f32[6,49152]{1,0:T(8,128)} copy(f32[6,49152]{1,0:T(8,128)S(1)} %pseudobands.1) | data formatting | bytes 2359296

commit v4 on v3

--- a/solution.py
+++ b/solution.py
@@ -19,8 +19,8 @@
 MERGE_LAG = 2
 NEAR_LAG = 3
 FAR_LAG = 4
-FINISH_LAG = 6
-UNPACK_LAG = 8
+FINISH_LAG = 7
+UNPACK_LAG = 11
 MESH = pl.DeviceIdType.MESH
 
 
@@ -473,10 +473,10 @@
             known += 1
         if 0 <= step - MERGE_LAG < count:
             merge(chunks[step - MERGE_LAG])
+        if 0 <= step - FAR_LAG < count:
+            finish(chunks[step - FAR_LAG], 1)
         if 0 <= step - NEAR_LAG < count:
             cross(chunks[step - NEAR_LAG], 0).start()
-        if 0 <= step - FAR_LAG < count:
-            finish(chunks[step - FAR_LAG], 1)
         if 0 <= step - FINISH_LAG < count:
             finish(chunks[step - FINISH_LAG], 0)
         if 0 <= step - UNPACK_LAG < count:

time: 48.1 us -> 47.7 us (level)
  no operation moved by 1% of the time
where the time goes in v4:
time: 47.7 us; the launch traced here: 47.6 us
  Pallas kernels  46.4 us (97%)
  local copies, waits for them, and re-layouts  1.15 us (2%)
    pallas_call x1, Pallas kernels, on_device(): pl.pallas_call(functools.partial(kernel, slabs, reach, chip_reach), out_s...  46.4 us
    unnamed x1, local copies, waits for them, and re-layouts  1.15 us

profile of v4, /device:TPU:0, one launch (start us, length us, event | category | flops | bytes accessed | tf_op | source)
XLA Modules:
  0.0 47.6 jit_solution(16059327610829124367)
XLA Ops:
  0.0 46.4 %pseudobands.1 = f32[6,49152]{1,0:T(8,128)S(1)} custom-call(s32[16]{0:T(128)} %widths_hbm.1, s32[16]{0:T(128)} %owner_hbm.1, s32[12,384]{1,0:T(8,128)} %signs_hbm.1, f32[384,12288]{1,0:T(8,128)} %band_ref.1), custom_call_target="tpu_custom_call" | custom-call | tf_op jit(solution)/shard_map/pseudobands/pallas_call | solution.py:530
  46.4 1.1 %copy.6 = f32[6,49152]{1,0:T(8,128)} copy(f32[6,49152]{1,0:T(8,128)S(1)} %pseudobands.1) | data formatting | bytes 2359296
